TPU v7x, 8 devices: a whole 2x2x1 slice. The times are simulated.
8 devices in a mesh: batch: 1 (over z), col: 2 (over y), row: 4 (over x, core).
Axes of the slice: x: 2, y: 2, z: 1, core: 2. Of those that a mesh axis runs over, the one named last changes fastest.
Arguments:
- pair_rep: bfloat16 [512, 512, 128], P(('batch', 'row'), 'col')
- pair_mask: int32 [512, 512], P(('batch', 'row'), 'col')
- ln_in_gain: bfloat16 [128], replicated
- proj_a: bfloat16 [128, 256], replicated
- gate_a: bfloat16 [128, 256], replicated
- proj_b: bfloat16 [128, 256], replicated
- gate_b: bfloat16 [128, 256], replicated
- gate_out: bfloat16 [128, 128], replicated
- proj_out: bfloat16 [256, 128], replicated
- ln_out_gain: bfloat16 [256], replicated
Outputs:
- output: bfloat16 [512, 512, 128], P(('batch', 'row'), 'col')
All inputs are finite; a program needn't handle non-finite values.
Results may differ from a plain program's by a relative error of at most 0.00477315.
Values are sent between devices in bfloat16 or wider.
A program may use at most 1 GiB of HBM per device.

v0:
```python
import jax
import jax.numpy as jnp
from jax import lax
from jax.sharding import PartitionSpec as P

LN_EPS = 1e-5


def layer_norm(values, gain):
    row_mean = jnp.mean(values, axis=-1, keepdims=True)
    centred = values - row_mean
    row_var = jnp.mean(centred * centred, axis=-1, keepdims=True)
    return centred * lax.rsqrt(row_var + LN_EPS) * gain.astype(jnp.float32)


def tile_front(z_tile, mask_tile, ln_in_gain, proj_a, gate_a, proj_b, gate_b, gate_out):
    x_norm = layer_norm(z_tile.astype(jnp.float32), ln_in_gain).astype(jnp.bfloat16)
    mask_f = mask_tile.astype(jnp.float32)[None]

    def gated_half(proj_w, gate_w):
        proj_val = jnp.einsum('dc,ijd->cij', proj_w, x_norm, preferred_element_type=jnp.float32)
        gate_val = jnp.einsum('dc,ijd->cij', gate_w, x_norm, preferred_element_type=jnp.float32)
        return (mask_f * jax.nn.sigmoid(gate_val) * proj_val).astype(jnp.bfloat16)

    left = gated_half(proj_a, gate_a)
    right = gated_half(proj_b, gate_b)
    out_gate = jax.nn.sigmoid(jnp.einsum('ijd,de->ije', x_norm, gate_out, preferred_element_type=jnp.float32))
    return left, right, out_gate


def tile_back(z_tile, tri_prod, out_gate, proj_out, ln_out_gain):
    chan_mean = jnp.mean(tri_prod, axis=0, keepdims=True)
    centred = tri_prod - chan_mean
    chan_var = jnp.mean(centred * centred, axis=0, keepdims=True)
    normed = (centred * lax.rsqrt(chan_var + LN_EPS) * ln_out_gain.astype(jnp.float32)[:, None, None]).astype(jnp.bfloat16)
    update = jnp.einsum('cij,cd->ijd', normed, proj_out, preferred_element_type=jnp.float32)
    return (z_tile.astype(jnp.float32) + out_gate * update).astype(jnp.bfloat16)


def solution(mesh):
    tile_spec = P(('batch', 'row'), 'col', None)
    mask_spec = P(('batch', 'row'), 'col')
    repl_spec = P()

    def per_device(z_tile, mask_tile, ln_in_gain, proj_a, gate_a, proj_b, gate_b, gate_out, proj_out, ln_out_gain):
        left, right, out_gate = tile_front(z_tile, mask_tile, ln_in_gain, proj_a, gate_a, proj_b, gate_b, gate_out)
        left_rows = lax.all_gather(left, 'col', axis=2, tiled=True)
        right_cols = lax.all_gather(right, 'row', axis=1, tiled=True)
        right_rows = lax.all_to_all(right_cols, 'col', 1, 2, tiled=True)
        tri_prod = jnp.einsum('cik,cjk->cij', left_rows, right_rows, preferred_element_type=jnp.float32)
        return tile_back(z_tile, tri_prod, out_gate, proj_out, ln_out_gain)

    return jax.shard_map(per_device, mesh=mesh, in_specs=(tile_spec, mask_spec) + (repl_spec,) * 8, out_specs=tile_spec, check_vma=False)
```

profile of v0, /device:TPU:5, one launch (start us, length us, event | category | flops | bytes accessed | tf_op | source)
XLA Modules:
  0.0 1928.8 jit_solution(5790054281922729761)
XLA Ops:
  6.5 0.0 copy-start
  6.5 0.0 copy-start.15
  6.5 0.0 copy-start.7
  6.5 0.0 all-gather.5.cloned.1.call-start
  6.5 5.7 convert_reduce_fusion
  12.3 0.0 copy-start.3
  12.3 0.0 slice-start
  12.3 10.9 fusion.2
  23.2 0.0 copy-done.15
  23.2 0.0 copy-start.5
  23.2 0.0 copy-done.7
  23.2 0.0 copy-start.10
  23.3 0.0 copy-done
  23.3 0.0 slice-start.1
  23.3 0.0 copy-start.12
  23.3 14.9 fusion.10
  38.2 0.0 slice-done
  38.2 0.0 slice-done.1
  38.2 0.0 copy-done.12
  38.2 19.6 %fusion.9 = bf16[256,128,256]{0,2,1:T(8,128)(2,1)} fusion(f32[128,256,256]{2,1,0:T(8,128)} %fusion.10, f32[128,256]{1,0:T(8,128)S(1)} %convert_element_type.31, bf16[128,256,128]{2,1,0:T(8,128)(2,1)S(1)} %bitcast.31, f32[128]{0:T(128)S(1)} %convert_element_type.29, f32[128,256]{1,0:T(8,128)S(1)} %add_rsqrt_fusion.1, ...), kind=kOutput, calls=%fused_computation.17 | convolution fusion | flops 2218786816 | bytes 59179520 | tf_op jit(solution)/shard_map/dc,ijd->cij/dot_general | solution.py:22
  57.8 22.3 %copy.14 = bf16[256,128,256]{2,0,1:T(8,128)(2,1)} copy(bf16[256,128,256]{0,2,1:T(8,128)(2,1)} %fusion.9) | data formatting | bytes 33554432 | tf_op jit(solution)/shard_map/convert_element_type | solution.py:23
  80.2 0.0 copy-start.8
  80.2 0.0 all-gather.5.cloned.1.call-update
  80.2 0.0 copy-start.13
  80.2 0.0 all-gather.3.cloned.1.call-start
  80.3 0.8 copy-done.8
  81.0 13.2 fusion.13
  94.2 0.0 copy-done.3
  94.2 0.0 copy-done.5
  94.2 0.0 copy-done.10
  94.2 0.0 copy-done.13
  94.3 17.4 fusion.8
  111.6 0.0 all-gather.3.cloned.1.call-update
  111.6 0.0 copy-start.16
  111.7 359.7 %all-gather.5.cloned.1.call-done = bf16[256,512,256]{2,0,1:T(8,128)(2,1)} async-done(((bf16[256,128,256]{2,0,1:T(8,128)(2,1)}), bf16[256,512,256]{2,0,1:T(8,128)(2,1)}) %all-gather.5.cloned.1.call-update) | async-done | bytes 67108880 | tf_op jit(solution)/shard_map/all_gather | solution.py:48
  471.4 25.7 %all-to-all-start = ((bf16[256,512,256]{2,0,1:T(8,128)(2,1)}), bf16[256,512,256]{2,0,1:T(8,128)(2,1)}, u32[]{:S(2)}, u32[]{:S(2)}) async-start(bf16[256,512,256]{2,0,1:T(8,128)(2,1)} %all-gather.5.cloned.1.call-done), calls=%async_computation | async-start | bytes 134217728 | tf_op jit(solution)/shard_map/all_to_all | solution.py:49
  497.0 0.0 copy-done.16
  497.1 718.0 %all-gather.3.cloned.1.call-done = bf16[256,128,512]{0,2,1:T(8,128)(2,1)} async-done(((bf16[256,128,256]{0,2,1:T(8,128)(2,1)}), bf16[256,128,512]{0,2,1:T(8,128)(2,1)}) %all-gather.3.cloned.1.call-update) | async-done | bytes 33554448 | tf_op jit(solution)/shard_map/all_gather | solution.py:47
  1215.0 44.9 %copy.16 = bf16[256,128,512]{2,1,0:T(8,128)(2,1)} copy(bf16[256,128,512]{0,2,1:T(8,128)(2,1)} %all-gather.3.cloned.1.call-done) | data formatting | bytes 67108864 | tf_op jit(solution)/shard_map/all_gather | solution.py:47
  1259.9 316.1 %all-to-all-done = bf16[256,512,256]{2,0,1:T(8,128)(2,1)} async-done(((bf16[256,512,256]{2,0,1:T(8,128)(2,1)}), bf16[256,512,256]{2,0,1:T(8,128)(2,1)}, u32[]{:S(2)}, u32[]{:S(2)}) %all-to-all-start) | async-done | bytes 67108896 | tf_op jit(solution)/shard_map/all_to_all | solution.py:49
  1576.1 119.2 %copy.21 = bf16[256,2,256,256]{3,1,2,0:T(2,128)(2,1)} copy(bf16[256,2,256,256]{3,0,2,1:T(8,128)(2,1)} %bitcast.7) | data formatting | bytes 134217728 | tf_op jit(solution)/shard_map/all_to_all | solution.py:49
  1695.3 104.3 %all_to_all.16 = bf16[256,256,512]{2,1,0:T(8,128)(2,1)} reshape(bf16[256,256,2,256]{3,2,1,0:T(2,128)(2,1)} %bitcast.29) | data formatting | bytes 134217728 | tf_op jit(solution)/shard_map/all_to_all | solution.py:49
  1799.6 46.1 %fusion.23 = (f32[128,256]{1,0:T(8,128)S(1)}, f32[256,128,256]{2,1,0:T(8,128)}) fusion(bf16[256,128,512]{2,1,0:T(8,128)(2,1)} %copy.16, bf16[256,256,512]{2,1,0:T(8,128)(2,1)} %all_to_all.16), kind=kOutput, calls=%fused_computation.30 | convolution fusion | flops 8598290432 | bytes 134348800 | tf_op jit(solution)/shard_map/cik,cjk->cij/dot_general | solution.py:50
  1845.7 0.0 copy-start.2
  1845.7 13.2 multiply_reduce_fusion
  1859.0 7.0 copy-done.2
  1866.0 0.0 copy-start.9
  1866.0 8.9 multiply_convert_fusion.2
  1874.9 0.0 copy-done.9
  1874.9 0.0 copy-start.4
  1874.9 0.0 copy-start.6
  1874.9 0.0 copy-start.11
  1874.9 0.0 copy-start.14
  1874.9 31.3 %fusion.6 = f32[128,256,128]{2,1,0:T(8,128)} fusion(bf16[256,128,256]{2,1,0:T(8,128)(2,1)} %multiply_convert_fusion.2, bf16[256,128]{1,0:T(8,128)(2,1)S(1)} %copy-done.9), kind=kOutput, calls=%fused_computation.14 | convolution fusion | flops 2147483648 | bytes 33619968 | tf_op jit(solution)/shard_map/cij,cd->ijd/dot_general | solution.py:36
  1906.2 0.0 copy-done.4
  1906.2 0.0 copy-done.6
  1906.2 0.0 copy-done.11
  1906.2 0.0 copy-done.14
  1906.2 0.0 copy-start.1
  1906.2 15.7 fusion.5
  1921.9 0.0 copy-done.1
  (8 shorter events, 0.1 us)
Async XLA Ops:
  6.5 16.7 copy-start
  6.5 16.7 copy-start.15
  6.5 16.7 copy-start.7
  6.5 464.8 %all-gather.5.cloned.1.call-start = ((), (), s32[]{:S(2)}) async-start(), calls=%async_computation.2 | async-start | bytes 83886080 | tf_op jit(solution)/shard_map/all_gather | solution.py:48
  12.3 81.9 %copy-start.3 = (f32[128,256]{1,0:T(8,128)}, f32[128,256]{1,0:T(8,128)S(1)}, u32[]{:S(2)}) copy-start(f32[128,256]{1,0:T(8,128)S(1)} %broadcast_multiply_fusion.1) | copy-start | bytes 393220
  12.3 25.9 %slice-start = ((s8[8388608]{0:T(1024)(128)(4,1)}), s8[4194304]{0:T(1024)(128)(4,1)S(1)}, s32[]{:S(2)}) async-start(s8[8388608]{0:T(1024)(128)(4,1)} %bitcast.30), calls=%async_computation.3 | async-start | bytes 8388608
  23.2 71.0 %copy-start.5 = (f32[128,256]{1,0:T(8,128)}, f32[128,256]{1,0:T(8,128)S(1)}, u32[]{:S(2)}) copy-start(f32[128,256]{1,0:T(8,128)S(1)} %add_rsqrt_fusion.1) | copy-start | bytes 393220
  23.2 71.0 %copy-start.10 = (f32[128]{0:T(128)}, f32[128]{0:T(128)S(1)}, u32[]{:S(2)}) copy-start(f32[128]{0:T(128)S(1)} %convert_element_type.29) | copy-start | bytes 1540
  23.3 14.9 slice-start.1
  23.3 14.9 copy-start.12
  80.2 0.8 copy-start.8
  80.2 14.1 copy-start.13
  80.2 1134.8 %all-gather.3.cloned.1.call-start = ((), (), s32[]{:S(2)}) async-start(), calls=%async_computation.1 | async-start | bytes 50331648 | tf_op jit(solution)/shard_map/all_gather | solution.py:47
  111.6 385.4 %copy-start.16 = (bf16[256]{0:T(256)(128)(2,1)S(1)}, bf16[256]{0:T(256)(128)(2,1)}, u32[]{:S(2)}) copy-start(bf16[256]{0:T(256)(128)(2,1)} %param.19) | copy-start | bytes 1540
  471.4 1104.7 %all-to-all-start = ((bf16[256,512,256]{2,0,1:T(8,128)(2,1)}), bf16[256,512,256]{2,0,1:T(8,128)(2,1)}, u32[]{:S(2)}, u32[]{:S(2)}) async-start(bf16[256,512,256]{2,0,1:T(8,128)(2,1)} %all-gather.5.cloned.1.call-done), calls=%async_computation | async-start | bytes 134217728 | tf_op jit(solution)/shard_map/all_to_all | solution.py:49
  1845.7 20.3 %copy-start.2 = (f32[256,128,256]{2,1,0:T(8,128)S(1)}, f32[256,128,256]{2,1,0:T(8,128)}, u32[]{:S(2)}) copy-start(f32[256,128,256]{2,1,0:T(8,128)} %get-tuple-element.6) | copy-start | bytes 100663296
  1866.0 8.9 copy-start.9
  1874.9 31.3 %copy-start.4 = (f32[128,256]{1,0:T(8,128)S(1)}, f32[128,256]{1,0:T(8,128)}, u32[]{:S(2)}) copy-start(f32[128,256]{1,0:T(8,128)} %copy-done.3) | copy-start | bytes 393220
  1874.9 31.3 %copy-start.6 = (f32[128,256]{1,0:T(8,128)S(1)}, f32[128,256]{1,0:T(8,128)}, u32[]{:S(2)}) copy-start(f32[128,256]{1,0:T(8,128)} %copy-done.5) | copy-start | bytes 393220
  1874.9 31.3 %copy-start.11 = (f32[128]{0:T(128)S(1)}, f32[128]{0:T(128)}, u32[]{:S(2)}) copy-start(f32[128]{0:T(128)} %copy-done.10) | copy-start | bytes 1540
  1874.9 31.3 %copy-start.14 = (bf16[128,128]{1,0:T(8,128)(2,1)S(1)}, bf16[128,128]{1,0:T(8,128)(2,1)}, u32[]{:S(2)}) copy-start(bf16[128,128]{1,0:T(8,128)(2,1)} %param.17) | copy-start | bytes 98308
  1906.2 15.7 copy-start.1
Sparse Core Ops, SparseCore 0:
  80.3 391.0 all-gather.4
  472.9 742.0 all-gather.2
where the time goes:
time: 1940 us; the launch traced here: 1930 us
  waiting for transfers between devices  1390 us (72%)
  local copies, waits for them, and re-layouts  299 us (15%)
  matrix products  158 us (8%)
  other arithmetic  38.8 us (2%)
  starting transfers between devices  25.7 us (1%)
    all_gather x1, waiting for transfers between devices, per_device(): left_rows = lax.all_gather(left, 'col', axis=2, tiled=True)  718 us
    all_gather x1, waiting for transfers between devices, per_device(): right_cols = lax.all_gather(right, 'row', axis=1, tiled=True)  360 us
    all_to_all x1, waiting for transfers between devices, per_device(): right_rows = lax.all_to_all(right_cols, 'col', 1, 2, tiled=True)  316 us
    all_to_all x2, local copies, waits for them, and re-layouts, per_device(): right_rows = lax.all_to_all(right_cols, 'col', 1, 2, tiled=True)  224 us
    dot_general x1, matrix products, per_device(): jnp.einsum('cik,cjk->cij', left_rows, right_rows, preferred_element_type=...  46.1 us
    all_gather x1, local copies, waits for them, and re-layouts, per_device(): left_rows = lax.all_gather(left, 'col', axis=2, tiled=True)  44.9 us
  transfers between devices with their start and end apart: 3, of which 3 were waited for; matrix products, arithmetic and copies ran while one was open for 4% of the time, Pallas kernels for 0%

commit v1 on v0

v1 whole, which is shorter than its diff:
```python
import jax
import jax.numpy as jnp
from jax import lax
from jax.experimental import pallas as pl
from jax.experimental.pallas import tpu as pltpu
from jax.sharding import PartitionSpec as P

LN_EPS = 1e-5
F32 = jnp.float32
BF16 = jnp.bfloat16
VMEM_LIMIT = 60 * 1024 * 1024
MESH = pl.DeviceIdType.MESH

ROWS, COLS, PAIR, HID = 128, 256, 128, 256
HALF = ROWS // 2
LANES = 128
FB = 16
NCH = ROWS // FB
NH = NCH // 2
CH = 128
PITCH = HID + 8
OPITCH = ROWS + 8
CB = 16
IB = 8
N_C, N_I = HID // CB, ROWS // IB


def normed_t(v, gain):
    mean = jnp.mean(v, axis=0, keepdims=True)
    cen = v - mean
    var = jnp.mean(cen * cen, axis=0, keepdims=True)
    return cen * lax.rsqrt(var + LN_EPS) * gain


def norm_chunk(z_ref, m_ref, first, gain, x_ref, xm_ref):
    for r in range(FB):
        z = z_ref[r].reshape(2, 2, HALF, PAIR)
        z = jnp.concatenate([z[0, 0], z[1, 0], z[0, 1], z[1, 1]], axis=0)
        x = normed_t(z.astype(F32).T, gain)
        x_ref[r] = x.astype(BF16)
        xm_ref[r] = (x * m_ref[pl.ds(first + r, 1), :].astype(F32)).astype(BF16)


def project_chunk(x_ref, w_ref, o_ref, scr):
    for r in range(FB):
        x = x_ref[r]
        for c in range(0, HID, CH):
            both = jnp.dot(w_ref[2 * c:2 * (c + CH), :], x, preferred_element_type=F32)
            proj = both[:CH]
            val = proj + jnp.tanh(both[CH:]) * proj
            for n in range(COLS // LANES):
                scr[n, pl.ds(r * PITCH + c, CH), :] = val[:, n * LANES:(n + 1) * LANES]

    def channel(c, _):
        for n in range(COLS // LANES):
            o_ref[c, :, n * LANES:(n + 1) * LANES] = scr[n, pl.ds(c, FB, stride=PITCH), :].astype(BF16)
        return 0

    lax.fori_loop(0, HID, channel, 0, unroll=16)


def back_body(step, a0, a1, b0, b1, z_ref, x_ref, o_ref, gate_ref, gain_ref, proj_ref, o_scr):
    @pl.when(step < N_C)
    def _():
        for c in range(CB):
            dims = (((1,), (1,)), ((), ()))
            acc = lax.dot_general(a0[0, c], b0[0, c], dims, preferred_element_type=F32)
            acc = acc + lax.dot_general(a1[0, c], b1[0, c], dims, preferred_element_type=F32)
            o_scr[pl.ds(pl.multiple_of((step * CB + c) * OPITCH, 8), ROWS), :] = acc

    @pl.when(step >= N_C)
    def _():
        first = (step - N_C) * IB
        gain = gain_ref[...]

        def one_row(i, _):
            tri = o_scr[pl.ds(first + i, HID, stride=OPITCH), :]
            y = normed_t(tri, gain).astype(BF16)
            u = jnp.dot(proj_ref[...], y, preferred_element_type=F32)
            g = jax.nn.sigmoid(jnp.dot(gate_ref[...], x_ref[i], preferred_element_type=F32))
            z = z_ref[i].reshape(2 * HALF, PAIR).astype(F32)
            o_ref[i] = (z + (g * u).T).astype(BF16).reshape(2, HALF, PAIR)
            return 0

        lax.fori_loop(0, IB, one_row, 0, unroll=4)


def back_specs(half):
    def chan(slot):
        return pl.BlockSpec((1, CB, ROWS, COLS), lambda s: (slot, jnp.minimum(s, N_C - 1), 0, 0))

    tile = pl.BlockSpec((IB, 2, HALF, PAIR), lambda s: (jnp.maximum(s - N_C, 0), 0, half, 0))
    x_spec = pl.BlockSpec((IB, PAIR, 2 * HALF), lambda s: (jnp.maximum(s - N_C, 0), 0, half))
    return [chan(0), chan(1), chan(2 + 2 * half), chan(3 + 2 * half), tile, x_spec], tile


def main_kernel(z_ref, z4_ref, mask_ref, gain_ref, w_ref, gate_ref, gout_ref, proj_ref,
                xb, g_ref, xt, out_ref,
                zbuf, xubuf, xmbuf, xin, obuf, scr, o_scr,
                zsem, xusem, xmsem, xsem, osem,
                y_s, p_s, q_s, s0_s, s1_s, y_r, p_r, q_r, s0_r, s1_r):
    row, col = lax.axis_index('row'), lax.axis_index('col')
    chip, core = row // 2, row % 2
    ydev = {'col': 1 - col}
    xdev = {'row': (1 - chip) * 2 + core}
    xydev = {'row': (1 - chip) * 2 + core, 'col': 1 - col}
    sdev = {'row': chip * 2 + 1 - core}
    diag = chip == col
    off = chip != col
    mine = 1 - diag.astype(jnp.int32)

    def part(k, slot, ch):
        return xb.at[k, slot, pl.ds(ch * FB, FB)]

    def rdma(src, dst, send, recv, dev):
        return pltpu.make_async_remote_copy(src_ref=src, dst_ref=dst, send_sem=send, recv_sem=recv,
                                            device_id=dev, device_id_type=MESH)

    def y(ch):
        return rdma(part(0, 0, ch), part(1, 0, ch), y_s.at[ch], y_r.at[ch], ydev)

    def p(ch):
        return rdma(part(0, 0, ch), part(0, 1, ch), p_s.at[ch], p_r.at[ch], xdev)

    def q_relay(ch):
        return rdma(part(1, 0, ch), part(1, 1, ch), q_s.at[ch], q_r.at[ch], xdev)

    def q_direct(ch):
        return rdma(part(0, 0, ch), part(1, 1, ch), q_s.at[ch], q_r.at[ch], xydev)

    def s0(ch):
        return rdma(part(0, mine, ch), part(0, 2, ch), s0_s.at[ch], s0_r.at[ch], sdev)

    def s1(ch):
        return rdma(part(1, mine, ch), part(1, 2, ch), s1_s.at[ch], s1_r.at[ch], sdev)

    barrier = pltpu.get_barrier_semaphore()
    for dev in (ydev, xdev, xydev, sdev):
        pl.semaphore_signal(barrier, inc=1, device_id=dev, device_id_type=MESH)

    def zload(ch):
        return pltpu.make_async_copy(z_ref.at[pl.ds(ch * FB, FB)], zbuf.at[ch % 2], zsem.at[ch % 2])

    def xustore(ch):
        return pltpu.make_async_copy(xubuf.at[ch % 2], xt.at[pl.ds(ch * FB, FB)], xusem.at[ch % 2])

    def xmstore(ch):
        return pltpu.make_async_copy(xmbuf.at[ch % 2], part(0, 0, ch), xmsem.at[ch % 2])

    def publish(ch):
        xmstore(ch).wait()
        y(ch).start()

        @pl.when(diag)
        def _():
            s0(ch).start()

        @pl.when(diag & (ch < NH))
        def _():
            p(ch).start()

    gain = gain_ref[...]
    zload(0).start()
    pl.semaphore_wait(barrier, 4)

    def norm_step(ch, _):
        @pl.when(ch + 1 < NCH)
        def _():
            zload(ch + 1).start()

        @pl.when(ch >= 2)
        def _():
            xustore(ch - 2).wait()

        zload(ch).wait()
        norm_chunk(zbuf.at[ch % 2], mask_ref, ch * FB, gain, xubuf.at[ch % 2], xmbuf.at[ch % 2])
        xustore(ch).start()
        xmstore(ch).start()

        @pl.when(ch >= 1)
        def _():
            publish(ch - 1)
        return 0

    lax.fori_loop(0, NCH, norm_step, 0)
    publish(NCH - 1)
    xustore(NCH - 2).wait()
    xustore(NCH - 1).wait()

    def xload(k, slot, ch, t):
        return pltpu.make_async_copy(part(k, slot, ch), xin.at[t], xsem.at[t])

    def ostore(dst, block, t):
        return pltpu.make_async_copy(obuf.at[t % 2], g_ref.at[dst, :, pl.ds(block * FB, FB), :], osem.at[t % 2])

    def project(first_use, t, weight, dst, block):
        @pl.when(jnp.logical_not(first_use))
        def _():
            ostore(0, 0, t).wait()
        project_chunk(xin.at[t], w_ref.at[weight], obuf.at[t % 2], scr)
        ostore(dst, block, t).start()

    def window1(i, _):
        k, ch = i // NH, i % NH
        y(i).wait_recv()

        @pl.when(diag)
        def _():
            s1(i).start()

        @pl.when(diag & (i < NH))
        def _():
            q_relay(i).start()

        @pl.when(diag & (i == NH - 1))
        def _():
            for c in range(NH, NCH):
                p(c).start()

        @pl.when(off & (i == NCH - 2))
        def _():
            for c in range(NH, NCH):
                q_direct(c).start()

        @pl.when(off & (i < NH))
        def _():
            p(ch).wait_recv()
            s0(ch).start()

        @pl.when(off & (i >= NH))
        def _():
            q_relay(ch).wait_recv()
            s1(ch).start()

        xload(0, 0, i, 0).start()
        xload(1, 0, i, 1).start()
        xload(k, mine, ch, 2).start()

        def step(t, _):
            @pl.when((t == 1) & (i < NH))
            def _():
                s0(ch).wait_recv()

            @pl.when((t == 1) & (i >= NH))
            def _():
                s1(ch).wait_recv()

            @pl.when(t == 1)
            def _():
                xload(k, 2, ch, 3).start()

            xload(0, 0, 0, t).wait()
            is_b = t // 2
            own_block = jnp.where(t == 2, core, 1 - core) * NH + ch
            project((i == 0) & (t < 2), t, is_b, jnp.where(is_b == 1, 2 + k, t), jnp.where(is_b == 1, own_block, i))
            return 0

        lax.fori_loop(0, 4, step, 0)
        return 0

    lax.fori_loop(0, NCH, window1, 0)
    ostore(0, 0, 0).wait()
    ostore(0, 0, 1).wait()

    specs, out_spec = back_specs(0)

    def pipe(a0, a1, b0, b1, zr, xr, o):
        back_body(pl.program_id(0), a0, a1, b0, b1, zr, xr, o, gate_ref, gout_ref, proj_ref, o_scr)

    pltpu.emit_pipeline(pipe, grid=(N_C + N_I,), in_specs=specs, out_specs=[out_spec])(
        g_ref, g_ref, g_ref, g_ref, z4_ref, xt, out_ref)

    def window2(i, _):
        ch = NH + i

        @pl.when(off)
        def _():
            p(ch).wait_recv()
            s0(ch).start()
            q_direct(ch).wait_recv()
            s1(ch).start()

        xload(0, mine, ch, 0).start()
        xload(1, mine, ch, 1).start()

        def step(t, _):
            @pl.when(t == 1)
            def _():
                s0(ch).wait_recv()
                xload(0, 2, ch, 2).start()
                s1(ch).wait_recv()
                xload(1, 2, ch, 3).start()

            xload(0, 0, 0, t).wait()
            project((i == 0) & (t < 2), t, 1, 4 + t % 2, jnp.where(t < 2, core, 1 - core) * NH + i)
            return 0

        lax.fori_loop(0, 4, step, 0)
        return 0

    lax.fori_loop(0, NCH - NH, window2, 0)
    ostore(0, 0, 0).wait()
    ostore(0, 0, 1).wait()

    def drain(ch, _):
        y(ch).wait_send()
        s0(ch).wait_send()
        s1(ch).wait_send()

        @pl.when(diag)
        def _():
            p(ch).wait_send()

        @pl.when(diag == (ch < NH))
        def _():
            q_direct(ch).wait_send()
        return 0

    lax.fori_loop(0, NCH, drain, 0)


def last_back_kernel(a0, a1, b0, b1, z_ref, x_ref, gate_ref, gain_ref, proj_ref, prev_ref, o_ref, o_scr):
    back_body(pl.program_id(0), a0, a1, b0, b1, z_ref, x_ref, o_ref, gate_ref, gain_ref, proj_ref, o_scr)


def solution(mesh):
    tile_spec = P(('batch', 'row'), 'col', None)
    mask_spec = P(('batch', 'row'), 'col')
    repl_spec = P()
    any_spec = pl.BlockSpec(memory_space=pl.ANY)
    vmem_spec = pl.BlockSpec(memory_space=pltpu.VMEM)
    dma = pltpu.SemaphoreType.DMA
    out4 = jax.ShapeDtypeStruct((ROWS, 2, 2 * HALF, PAIR), BF16)

    def per_device(z_tile, mask_tile, ln_in_gain, proj_a, gate_a, proj_b, gate_b, gate_out, proj_out, ln_out_gain):
        mask = mask_tile.reshape(ROWS, 2, 2, HALF).transpose(0, 2, 1, 3).reshape(ROWS, COLS)
        gain_in = ln_in_gain.astype(F32).reshape(PAIR, 1)
        gain_out = ln_out_gain.astype(F32).reshape(HID, 1)
        z4 = z_tile.reshape(ROWS, 2, 2 * HALF, PAIR)

        def weights(proj, gate):
            both = jnp.stack([proj.T.reshape(HID // CH, CH, PAIR), gate.T.reshape(HID // CH, CH, PAIR)], axis=1)
            return both.reshape(2 * HID, PAIR) * 0.5

        w = jnp.stack([weights(proj_a, gate_a), weights(proj_b, gate_b)])
        gate_t, proj_t = gate_out.T, proj_out.T

        xb, g, xt, out = pl.pallas_call(
            main_kernel,
            out_shape=(
                jax.ShapeDtypeStruct((2, 3, ROWS, PAIR, COLS), BF16),
                jax.ShapeDtypeStruct((6, HID, ROWS, COLS), BF16),
                jax.ShapeDtypeStruct((ROWS, PAIR, COLS), BF16),
                out4,
            ),
            in_specs=[any_spec, any_spec] + [vmem_spec] * 6,
            out_specs=(any_spec,) * 4,
            scratch_shapes=[
                pltpu.VMEM((2, FB, COLS, PAIR), BF16),
                pltpu.VMEM((2, FB, PAIR, COLS), BF16),
                pltpu.VMEM((2, FB, PAIR, COLS), BF16),
                pltpu.VMEM((4, FB, PAIR, COLS), BF16),
                pltpu.VMEM((2, HID, FB, COLS), BF16),
                pltpu.VMEM((COLS // LANES, FB * PITCH, LANES), F32),
                pltpu.VMEM((HID * OPITCH, 2 * HALF), F32),
                dma((2,)), dma((2,)), dma((2,)), dma((4,)), dma((2,)),
            ] + [dma((NCH,))] * 10,
            compiler_params=pltpu.CompilerParams(vmem_limit_bytes=VMEM_LIMIT, collective_id=0, has_side_effects=True),
            name='exchange_project',
        )(z_tile, z4, mask, gain_in, w, gate_t, gain_out, proj_t)

        def whole(*shape):
            return pl.BlockSpec(shape, lambda s: (0,) * len(shape))

        specs, out_spec = back_specs(1)
        out = pl.pallas_call(
            last_back_kernel,
            grid=(N_C + N_I,),
            out_shape=out4,
            in_specs=specs + [whole(PAIR, PAIR), whole(HID, 1), whole(PAIR, HID), any_spec],
            out_specs=out_spec,
            scratch_shapes=[pltpu.VMEM((HID * OPITCH, 2 * HALF), F32)],
            input_output_aliases={9: 0},
            compiler_params=pltpu.CompilerParams(vmem_limit_bytes=VMEM_LIMIT),
            name='back',
        )(g, g, g, g, z4, xt, gate_t, gain_out, proj_t, out)
        return out.reshape(ROWS, COLS, PAIR)

    return jax.shard_map(per_device, mesh=mesh, in_specs=(tile_spec, mask_spec) + (repl_spec,) * 8, out_specs=tile_spec, check_vma=False)
```

time: 1940 us -> 443 us (0.23)
  waiting for transfers between devices: 1390 us -> 0 us
  Pallas kernels: 0 us -> 421 us
  local copies, waits for them, and re-layouts: 299 us -> 18 us
  matrix products: 158 us -> 0 us
  other arithmetic: 38.8 us -> 2.08 us
  starting transfers between devices: 25.7 us -> 0 us
    all_gather x2 -> x0, waiting for transfers between devices: 1080 us -> none  [the longest x1 718 us: per_device(): left_rows = lax.all_gather(left, 'col', axis=2, tiled=True)]
    pallas_call x0 -> x2, Pallas kernels: none -> 421 us  [the longest x1 376 us: per_device(): pl.pallas_call(main_kernel, out_shape=(jax.ShapeDtypeStruct((2, 3, ROWS,...]
    all_to_all x1 -> x0, waiting for transfers between devices: 316 us -> none  [per_device(): right_rows = lax.all_to_all(right_cols, 'col', 1, 2, tiled=True)]
    all_to_all x2 -> x0, local copies, waits for them, and re-layouts: 224 us -> none  [per_device(): right_rows = lax.all_to_all(right_cols, 'col', 1, 2, tiled=True)]
    dot_general x7 -> x0, matrix products: 158 us -> none  [the longest x1 46.1 us: per_device(): jnp.einsum('cik,cjk->cij', left_rows, right_rows, preferred_element_type=...]
    all_gather x1 -> x0, local copies, waits for them, and re-layouts: 44.9 us -> none  [per_device(): left_rows = lax.all_gather(left, 'col', axis=2, tiled=True)]
    reduce_sum x3 -> x0, other arithmetic: 29.8 us -> none  [the longest x1 13.2 us: tile_back(): chan_var = jnp.mean(centred * centred, axis=0, keepdims=True)]
    all_to_all x1 -> x0, starting transfers between devices: 25.7 us -> none  [per_device(): right_rows = lax.all_to_all(right_cols, 'col', 1, 2, tiled=True)]
  transfers between devices with their start and end apart: 3 -> 0, of which waited for: 3 -> 0; matrix products, arithmetic and copies ran while one was open for 4% -> 0% of each run, Pallas kernels for 0% -> 0%
where the time goes in v1:
time: 443 us; the launch traced here: 441 us
  Pallas kernels  421 us (95%)
  local copies, waits for them, and re-layouts  18 us (4%)
    pallas_call x1, Pallas kernels, per_device(): pl.pallas_call(main_kernel, out_shape=(jax.ShapeDtypeStruct((2, 3, ROWS,...  376 us
    pallas_call x1, Pallas kernels, per_device(): pl.pallas_call(last_back_kernel, grid=(N_C + N_I,), out_shape=out4, in_sp...  44.6 us
    unnamed x4, local copies, waits for them, and re-layouts  11.9 us

profile of v1, /device:TPU:5, one launch (start us, length us, event | category | flops | bytes accessed | tf_op | source)
XLA Modules:
  0.0 441.1 jit_solution(6077021876769916922)
XLA Ops:
  0.0 0.7 bitcast_convert_fusion
  0.7 0.7 reshape.58
  1.3 1.5 copy.26
  2.8 0.7 copy.29.gain_ref
  3.5 0.9 copy.32
  4.5 1.0 copy.33
  5.5 1.0 copy.34
  6.4 1.0 copy.35
  7.4 0.7 pad_maximum_fusion.w_ref
  8.1 1.6 copy.27
  9.7 0.8 copy.30.gout_ref.gain_ref
  10.5 1.0 copy.20
  11.5 0.8 copy.28.mask_ref
  12.3 376.3 %exchange_project.1 = (bf16[2,3,128,128,256]{4,3,2,1,0:T(8,128)(2,1)}, bf16[6,256,128,256]{3,2,1,0:T(8,128)(2,1)}, bf16[128,128,256]{2,1,0:T(8,128)(2,1)}, bf16[128,2,128,128]{3,2,1,0:T(8,128)(2,1)}) custom-call(bf16[128,256,128]{2,1,0:T(8,128)(2,1)} %z_ref.1, bf16[128,2,128,128]{3,2,1,0:T(8,128)(2,1)} %bitcast.22, s32[128,256]{1,0:T(8,128)} %copy.28.mask_ref, ...), custom_call_target="tpu_custom_call" | custom-call | tf_op jit(solution)/shard_map/exchange_project/pallas_call | solution.py:348
  388.6 44.6 %back.1 = bf16[128,2,128,128]{3,2,1,0:T(8,128)(2,1)} custom-call(bf16[6,256,128,256]{3,2,1,0:T(8,128)(2,1)} %get-tuple-element.8.a0.a1.b0.b1, bf16[6,256,128,256]{3,2,1,0:T(8,128)(2,1)} %get-tuple-element.8.a0.a1.b0.b1, bf16[6,256,128,256]{3,2,1,0:T(8,128)(2,1)} %get-tuple-element.8.a0.a1.b0.b1, ...), custom_call_target="tpu_custom_call", output_to_operand_aliasing={{}: (9, {})} | custom-call | tf_op jit(solution)/shard_map/back/pallas_call | solution.py:376
  433.2 7.9 %copy.38 = bf16[128,256,128]{2,1,0:T(8,128)(2,1)} copy(bf16[128,256,128]{2,1,0:T(8,128)(2,1)} %bitcast.24) | data formatting | bytes 16777216
  (3 shorter events, 0.1 us)

commit v2 on v1

--- a/solution.py
+++ b/solution.py
@@ -59,6 +59,16 @@
     lax.fori_loop(0, HID, channel, 0, unroll=16)
 
 
+def column(row_ref):
+    return row_ref[...].astype(F32).reshape(1, -1).T
+
+
+def out_weights(gate_ref, gain_ref, proj_ref, gate_t, gain, proj_t):
+    gate_t[...] = gate_ref[...].astype(F32).T.astype(BF16)
+    gain[...] = column(gain_ref)
+    proj_t[...] = proj_ref[...].astype(F32).T.astype(BF16)
+
+
 def back_body(step, a0, a1, b0, b1, z_ref, x_ref, o_ref, gate_ref, gain_ref, proj_ref, o_scr):
     @pl.when(step < N_C)
     def _():
@@ -79,7 +89,7 @@
             u = jnp.dot(proj_ref[...], y, preferred_element_type=F32)
             g = jax.nn.sigmoid(jnp.dot(gate_ref[...], x_ref[i], preferred_element_type=F32))
             z = z_ref[i].reshape(2 * HALF, PAIR).astype(F32)
-            o_ref[i] = (z + (g * u).T).astype(BF16).reshape(2, HALF, PAIR)
+            o_ref[i, :, o_ref.shape[2] - HALF:] = (z + (g * u).T).astype(BF16).reshape(2, HALF, PAIR)
             return 0
 
         lax.fori_loop(0, IB, one_row, 0, unroll=4)
@@ -90,20 +100,20 @@
         return pl.BlockSpec((1, CB, ROWS, COLS), lambda s: (slot, jnp.minimum(s, N_C - 1), 0, 0))
 
     tile = pl.BlockSpec((IB, 2, HALF, PAIR), lambda s: (jnp.maximum(s - N_C, 0), 0, half, 0))
+    first = pl.BlockSpec((IB, 2, HALF, PAIR), lambda s: (jnp.maximum(s - N_C, 0), 0, 0, 0))
     x_spec = pl.BlockSpec((IB, PAIR, 2 * HALF), lambda s: (jnp.maximum(s - N_C, 0), 0, half))
-    return [chan(0), chan(1), chan(2 + 2 * half), chan(3 + 2 * half), tile, x_spec], tile
-
-
-def main_kernel(z_ref, z4_ref, mask_ref, gain_ref, w_ref, gate_ref, gout_ref, proj_ref,
+    return [chan(0), chan(1), chan(2 + 2 * half), chan(3 + 2 * half), tile, x_spec], first
+
+
+def main_kernel(z_ref, z4_ref, mask_in, gain_in, proj_a, gate_a, proj_b, gate_b, gate_in, gout_in, proj_in,
                 xb, g_ref, xt, out_ref,
-                zbuf, xubuf, xmbuf, xin, obuf, scr, o_scr,
+                mask_ref, w_ref, gate_ref, gout_ref, proj_ref, zbuf, xubuf, xmbuf, xin, obuf, scr, o_scr,
                 zsem, xusem, xmsem, xsem, osem,
                 y_s, p_s, q_s, s0_s, s1_s, y_r, p_r, q_r, s0_r, s1_r):
     row, col = lax.axis_index('row'), lax.axis_index('col')
     chip, core = row // 2, row % 2
     ydev = {'col': 1 - col}
     xdev = {'row': (1 - chip) * 2 + core}
-    xydev = {'row': (1 - chip) * 2 + core, 'col': 1 - col}
     sdev = {'row': chip * 2 + 1 - core}
     diag = chip == col
     off = chip != col
@@ -125,8 +135,11 @@
     def q_relay(ch):
         return rdma(part(1, 0, ch), part(1, 1, ch), q_s.at[ch], q_r.at[ch], xdev)
 
-    def q_direct(ch):
-        return rdma(part(0, 0, ch), part(1, 1, ch), q_s.at[ch], q_r.at[ch], xydev)
+    def q_hop(ch):
+        return rdma(part(0, 0, ch), part(1, 1, ch), q_s.at[ch], q_r.at[ch], xdev)
+
+    def q_hop2(ch):
+        return rdma(part(1, 1, ch), part(1, 1, ch), q_s.at[ch], q_r.at[ch], ydev)
 
     def s0(ch):
         return rdma(part(0, mine, ch), part(0, 2, ch), s0_s.at[ch], s0_r.at[ch], sdev)
@@ -135,7 +148,7 @@
         return rdma(part(1, mine, ch), part(1, 2, ch), s1_s.at[ch], s1_r.at[ch], sdev)
 
     barrier = pltpu.get_barrier_semaphore()
-    for dev in (ydev, xdev, xydev, sdev):
+    for dev in (ydev, xdev, sdev):
         pl.semaphore_signal(barrier, inc=1, device_id=dev, device_id_type=MESH)
 
     def zload(ch):
@@ -159,9 +172,15 @@
         def _():
             p(ch).start()
 
-    gain = gain_ref[...]
+        @pl.when(off & (ch >= NH))
+        def _():
+            q_hop(ch).start()
+
     zload(0).start()
-    pl.semaphore_wait(barrier, 4)
+    gain = column(gain_in)
+    mask = mask_in[...]
+    mask_ref[...] = jnp.concatenate([mask[:, n * HALF:(n + 1) * HALF] for n in (0, 2, 1, 3)], axis=1)
+    pl.semaphore_wait(barrier, 3)
 
     def norm_step(ch, _):
         @pl.when(ch + 1 < NCH)
@@ -187,6 +206,13 @@
     xustore(NCH - 2).wait()
     xustore(NCH - 1).wait()
 
+    for n, (proj, gate) in enumerate(((proj_a, gate_a), (proj_b, gate_b))):
+        for half, ref in ((0, proj), (1, gate)):
+            w_t = (ref[...].astype(F32).T * 0.5).astype(BF16)
+            for c in range(HID // CH):
+                w_ref[n, pl.ds((2 * c + half) * CH, CH), :] = w_t[c * CH:(c + 1) * CH]
+    out_weights(gate_in, gout_in, proj_in, gate_ref, gout_ref, proj_ref)
+
     def xload(k, slot, ch, t):
         return pltpu.make_async_copy(part(k, slot, ch), xin.at[t], xsem.at[t])
 
@@ -217,10 +243,10 @@
             for c in range(NH, NCH):
                 p(c).start()
 
-        @pl.when(off & (i == NCH - 2))
-        def _():
-            for c in range(NH, NCH):
-                q_direct(c).start()
+        @pl.when(diag & (i >= NH))
+        def _():
+            q_hop(i).wait_recv()
+            q_hop2(i).start()
 
         @pl.when(off & (i < NH))
         def _():
@@ -277,7 +303,7 @@
         def _():
             p(ch).wait_recv()
             s0(ch).start()
-            q_direct(ch).wait_recv()
+            q_hop2(ch).wait_recv()
             s1(ch).start()
 
         xload(0, mine, ch, 0).start()
@@ -311,16 +337,25 @@
         def _():
             p(ch).wait_send()
 
-        @pl.when(diag == (ch < NH))
-        def _():
-            q_direct(ch).wait_send()
+        @pl.when(diag | (ch >= NH))
+        def _():
+            q_hop(ch).wait_send()
         return 0
 
     lax.fori_loop(0, NCH, drain, 0)
 
 
-def last_back_kernel(a0, a1, b0, b1, z_ref, x_ref, gate_ref, gain_ref, proj_ref, prev_ref, o_ref, o_scr):
-    back_body(pl.program_id(0), a0, a1, b0, b1, z_ref, x_ref, o_ref, gate_ref, gain_ref, proj_ref, o_scr)
+def last_back_kernel(a0, a1, b0, b1, z_ref, x_ref, gate_ref, gain_ref, proj_ref, first_ref, o_ref, gate_t, gain, proj_t, o_scr):
+    step = pl.program_id(0)
+
+    @pl.when(step == 0)
+    def _():
+        out_weights(gate_ref, gain_ref, proj_ref, gate_t, gain, proj_t)
+
+    @pl.when(step >= N_C)
+    def _():
+        o_ref[:, :, :HALF] = first_ref[...]
+    back_body(step, a0, a1, b0, b1, z_ref, x_ref, o_ref, gate_t, gain, proj_t, o_scr)
 
 
 def solution(mesh):
@@ -330,32 +365,26 @@
     any_spec = pl.BlockSpec(memory_space=pl.ANY)
     vmem_spec = pl.BlockSpec(memory_space=pltpu.VMEM)
     dma = pltpu.SemaphoreType.DMA
-    out4 = jax.ShapeDtypeStruct((ROWS, 2, 2 * HALF, PAIR), BF16)
 
     def per_device(z_tile, mask_tile, ln_in_gain, proj_a, gate_a, proj_b, gate_b, gate_out, proj_out, ln_out_gain):
-        mask = mask_tile.reshape(ROWS, 2, 2, HALF).transpose(0, 2, 1, 3).reshape(ROWS, COLS)
-        gain_in = ln_in_gain.astype(F32).reshape(PAIR, 1)
-        gain_out = ln_out_gain.astype(F32).reshape(HID, 1)
+        gain_in, gain_out = ln_in_gain.reshape(1, PAIR), ln_out_gain.reshape(1, HID)
         z4 = z_tile.reshape(ROWS, 2, 2 * HALF, PAIR)
-
-        def weights(proj, gate):
-            both = jnp.stack([proj.T.reshape(HID // CH, CH, PAIR), gate.T.reshape(HID // CH, CH, PAIR)], axis=1)
-            return both.reshape(2 * HID, PAIR) * 0.5
-
-        w = jnp.stack([weights(proj_a, gate_a), weights(proj_b, gate_b)])
-        gate_t, proj_t = gate_out.T, proj_out.T
-
-        xb, g, xt, out = pl.pallas_call(
+        out_w = [pltpu.VMEM((PAIR, PAIR), BF16), pltpu.VMEM((HID, 1), F32), pltpu.VMEM((PAIR, HID), BF16)]
+
+        _, g, xt, first = pl.pallas_call(
             main_kernel,
             out_shape=(
                 jax.ShapeDtypeStruct((2, 3, ROWS, PAIR, COLS), BF16),
                 jax.ShapeDtypeStruct((6, HID, ROWS, COLS), BF16),
                 jax.ShapeDtypeStruct((ROWS, PAIR, COLS), BF16),
-                out4,
+                jax.ShapeDtypeStruct((ROWS, 2, HALF, PAIR), BF16),
             ),
-            in_specs=[any_spec, any_spec] + [vmem_spec] * 6,
+            in_specs=[any_spec, any_spec] + [vmem_spec] * 9,
             out_specs=(any_spec,) * 4,
             scratch_shapes=[
+                pltpu.VMEM((ROWS, COLS), jnp.int32),
+                pltpu.VMEM((2, 2 * HID, PAIR), BF16),
+                *out_w,
                 pltpu.VMEM((2, FB, COLS, PAIR), BF16),
                 pltpu.VMEM((2, FB, PAIR, COLS), BF16),
                 pltpu.VMEM((2, FB, PAIR, COLS), BF16),
@@ -367,23 +396,22 @@
             ] + [dma((NCH,))] * 10,
             compiler_params=pltpu.CompilerParams(vmem_limit_bytes=VMEM_LIMIT, collective_id=0, has_side_effects=True),
             name='exchange_project',
-        )(z_tile, z4, mask, gain_in, w, gate_t, gain_out, proj_t)
+        )(z_tile, z4, mask_tile, gain_in, proj_a, gate_a, proj_b, gate_b, gate_out, gain_out, proj_out)
 
         def whole(*shape):
             return pl.BlockSpec(shape, lambda s: (0,) * len(shape))
 
-        specs, out_spec = back_specs(1)
+        specs, first_spec = back_specs(1)
         out = pl.pallas_call(
             last_back_kernel,
             grid=(N_C + N_I,),
-            out_shape=out4,
-            in_specs=specs + [whole(PAIR, PAIR), whole(HID, 1), whole(PAIR, HID), any_spec],
-            out_specs=out_spec,
-            scratch_shapes=[pltpu.VMEM((HID * OPITCH, 2 * HALF), F32)],
-            input_output_aliases={9: 0},
+            out_shape=jax.ShapeDtypeStruct((ROWS, 2, 2 * HALF, PAIR), BF16),
+            in_specs=specs + [whole(PAIR, PAIR), whole(1, HID), whole(HID, PAIR), first_spec],
+            out_specs=pl.BlockSpec((IB, 2, 2 * HALF, PAIR), lambda s: (jnp.maximum(s - N_C, 0), 0, 0, 0)),
+            scratch_shapes=[*out_w, pltpu.VMEM((HID * OPITCH, 2 * HALF), F32)],
             compiler_params=pltpu.CompilerParams(vmem_limit_bytes=VMEM_LIMIT),
             name='back',
-        )(g, g, g, g, z4, xt, gate_t, gain_out, proj_t, out)
+        )(g, g, g, g, z4, xt, gate_out, gain_out, proj_out, first)
         return out.reshape(ROWS, COLS, PAIR)
 
     return jax.shard_map(per_device, mesh=mesh, in_specs=(tile_spec, mask_spec) + (repl_spec,) * 8, out_specs=tile_spec, check_vma=False)

time: 443 us -> 338 us (0.76)
  Pallas kernels: 421 us -> 335 us
  local copies, waits for them, and re-layouts: 18 us -> 1.24 us
    pallas_call x1, Pallas kernels: 376 us -> 289 us  [per_device(): pl.pallas_call(main_kernel, out_shape=(jax.ShapeDtypeStruct((2, 3, ROWS,...]
    unnamed x4 -> x0, local copies, waits for them, and re-layouts: 11.9 us -> none
where the time goes in v2:
time: 338 us; the launch traced here: 337 us
  Pallas kernels  335 us (99%)
    pallas_call x1, Pallas kernels, per_device(): pl.pallas_call(main_kernel, out_shape=(jax.ShapeDtypeStruct((2, 3, ROWS,...  289 us
    pallas_call x1, Pallas kernels, per_device(): pl.pallas_call(last_back_kernel, grid=(N_C + N_I,), out_shape=jax.ShapeDt...  45.9 us

profile of v2, /device:TPU:5, one launch (start us, length us, event | category | flops | bytes accessed | tf_op | source)
XLA Modules:
  0.0 336.6 jit_solution(2195980742250518984)
XLA Ops:
  0.0 1.2 reshape.14.gout_in.gain_ref
  1.2 289.5 %exchange_project.1 = (bf16[2,3,128,128,256]{4,3,2,1,0:T(8,128)(2,1)}, bf16[6,256,128,256]{3,2,1,0:T(8,128)(2,1)}, bf16[128,128,256]{2,1,0:T(8,128)(2,1)}, bf16[128,2,64,128]{3,2,1,0:T(8,128)(2,1)}) custom-call(bf16[128,256,128]{2,1,0:T(8,128)(2,1)} %z_ref.1, bf16[128,2,128,128]{3,2,1,0:T(8,128)(2,1)} %bitcast.3, s32[128,256]{1,0:T(8,128)} %mask_in.1, ...), custom_call_target="tpu_custom_call" | custom-call | tf_op jit(solution)/shard_map/exchange_project/pallas_call | solution.py:374
  290.7 45.9 %back.1 = bf16[128,2,128,128]{3,2,1,0:T(8,128)(2,1)} custom-call(bf16[6,256,128,256]{3,2,1,0:T(8,128)(2,1)} %get-tuple-element.8.a0.a1.b0.b1, bf16[6,256,128,256]{3,2,1,0:T(8,128)(2,1)} %get-tuple-element.8.a0.a1.b0.b1, bf16[6,256,128,256]{3,2,1,0:T(8,128)(2,1)} %get-tuple-element.8.a0.a1.b0.b1, bf16[6,256,128,256]{3,2,1,0:T(8,128)(2,1)} %get-tuple-element.8.a0.a1.b0.b1, ...), custom_call_target="tpu_custom_call" | custom-call | tf_op jit(solution)/shard_map/back/pallas_call | solution.py:405

commit v3 on v2

--- a/solution.py
+++ b/solution.py
@@ -18,10 +18,10 @@
 NCH = ROWS // FB
 NH = NCH // 2
 CH = 128
-PITCH = HID + 8
+PITCH = HID + 4
 OPITCH = ROWS + 8
-CB = 16
-IB = 8
+CB = 32
+IB = 16
 N_C, N_I = HID // CB, ROWS // IB
 
 
@@ -92,7 +92,7 @@
             o_ref[i, :, o_ref.shape[2] - HALF:] = (z + (g * u).T).astype(BF16).reshape(2, HALF, PAIR)
             return 0
 
-        lax.fori_loop(0, IB, one_row, 0, unroll=4)
+        lax.fori_loop(0, IB, one_row, 0, unroll=16)
 
 
 def back_specs(half):

time: 338 us -> 326 us (0.964)
  Pallas kernels: 335 us -> 324 us
    pallas_call x1, Pallas kernels: 45.9 us -> 35.8 us  [per_device(): pl.pallas_call(last_back_kernel, grid=(N_C + N_I,), out_shape=jax.ShapeDt...]
where the time goes in v3:
time: 326 us; the launch traced here: 325 us
  Pallas kernels  324 us (99%)
    pallas_call x1, Pallas kernels, per_device(): pl.pallas_call(main_kernel, out_shape=(jax.ShapeDtypeStruct((2, 3, ROWS,...  288 us
    pallas_call x1, Pallas kernels, per_device(): pl.pallas_call(last_back_kernel, grid=(N_C + N_I,), out_shape=jax.ShapeDt...  35.8 us

profile of v3, /device:TPU:5, one launch (start us, length us, event | category | flops | bytes accessed | tf_op | source)
XLA Modules:
  0.0 325.2 jit_solution(6294896867770013096)
XLA Ops:
  0.0 1.2 reshape.14.gout_in.gain_ref
  1.2 288.2 %exchange_project.1 = (bf16[2,3,128,128,256]{4,3,2,1,0:T(8,128)(2,1)}, bf16[6,256,128,256]{3,2,1,0:T(8,128)(2,1)}, bf16[128,128,256]{2,1,0:T(8,128)(2,1)}, bf16[128,2,64,128]{3,2,1,0:T(8,128)(2,1)}) custom-call(bf16[128,256,128]{2,1,0:T(8,128)(2,1)} %z_ref.1, bf16[128,2,128,128]{3,2,1,0:T(8,128)(2,1)} %bitcast.3, s32[128,256]{1,0:T(8,128)} %mask_in.1, ...), custom_call_target="tpu_custom_call" | custom-call | tf_op jit(solution)/shard_map/exchange_project/pallas_call | solution.py:374
  289.4 35.8 %back.1 = bf16[128,2,128,128]{3,2,1,0:T(8,128)(2,1)} custom-call(bf16[6,256,128,256]{3,2,1,0:T(8,128)(2,1)} %get-tuple-element.8.a0.a1.b0.b1, bf16[6,256,128,256]{3,2,1,0:T(8,128)(2,1)} %get-tuple-element.8.a0.a1.b0.b1, bf16[6,256,128,256]{3,2,1,0:T(8,128)(2,1)} %get-tuple-element.8.a0.a1.b0.b1, bf16[6,256,128,256]{3,2,1,0:T(8,128)(2,1)} %get-tuple-element.8.a0.a1.b0.b1, ...), custom_call_target="tpu_custom_call" | custom-call | tf_op jit(solution)/shard_map/back/pallas_call | solution.py:405

commit v4 on v3

--- a/solution.py
+++ b/solution.py
@@ -19,7 +19,7 @@
 NH = NCH // 2
 CH = 128
 PITCH = HID + 4
-OPITCH = ROWS + 8
+OPITCH = ROWS + 4
 CB = 32
 IB = 16
 N_C, N_I = HID // CB, ROWS // IB
@@ -60,13 +60,14 @@
 
 
 def column(row_ref):
-    return row_ref[...].astype(F32).reshape(1, -1).T
+    cols = row_ref[...].astype(F32).T
+    return jnp.concatenate([cols[:, n:n + 1] for n in range(cols.shape[1])], axis=0)
 
 
 def out_weights(gate_ref, gain_ref, proj_ref, gate_t, gain, proj_t):
-    gate_t[...] = gate_ref[...].astype(F32).T.astype(BF16)
+    gate_t[...] = (gate_ref[...].astype(F32).T * 0.5).astype(BF16)
     gain[...] = column(gain_ref)
-    proj_t[...] = proj_ref[...].astype(F32).T.astype(BF16)
+    proj_t[...] = (proj_ref[...].astype(F32).T * 0.5).astype(BF16)
 
 
 def back_body(step, a0, a1, b0, b1, z_ref, x_ref, o_ref, gate_ref, gain_ref, proj_ref, o_scr):
@@ -76,7 +77,7 @@
             dims = (((1,), (1,)), ((), ()))
             acc = lax.dot_general(a0[0, c], b0[0, c], dims, preferred_element_type=F32)
             acc = acc + lax.dot_general(a1[0, c], b1[0, c], dims, preferred_element_type=F32)
-            o_scr[pl.ds(pl.multiple_of((step * CB + c) * OPITCH, 8), ROWS), :] = acc
+            o_scr[pl.ds(pl.multiple_of((step * CB + c) * OPITCH, 4), ROWS), :] = acc
 
     @pl.when(step >= N_C)
     def _():
@@ -87,9 +88,9 @@
             tri = o_scr[pl.ds(first + i, HID, stride=OPITCH), :]
             y = normed_t(tri, gain).astype(BF16)
             u = jnp.dot(proj_ref[...], y, preferred_element_type=F32)
-            g = jax.nn.sigmoid(jnp.dot(gate_ref[...], x_ref[i], preferred_element_type=F32))
+            t = jnp.tanh(jnp.dot(gate_ref[...], x_ref[i], preferred_element_type=F32))
             z = z_ref[i].reshape(2 * HALF, PAIR).astype(F32)
-            o_ref[i, :, o_ref.shape[2] - HALF:] = (z + (g * u).T).astype(BF16).reshape(2, HALF, PAIR)
+            o_ref[i, :, o_ref.shape[2] - HALF:] = (z + (u + t * u).T).astype(BF16).reshape(2, HALF, PAIR)
             return 0
 
         lax.fori_loop(0, IB, one_row, 0, unroll=16)
@@ -196,7 +197,11 @@
         xustore(ch).start()
         xmstore(ch).start()
 
-        @pl.when(ch >= 1)
+        @pl.when(ch == 0)
+        def _():
+            publish(0)
+
+        @pl.when(ch >= 2)
         def _():
             publish(ch - 1)
         return 0
@@ -367,7 +372,7 @@
     dma = pltpu.SemaphoreType.DMA
 
     def per_device(z_tile, mask_tile, ln_in_gain, proj_a, gate_a, proj_b, gate_b, gate_out, proj_out, ln_out_gain):
-        gain_in, gain_out = ln_in_gain.reshape(1, PAIR), ln_out_gain.reshape(1, HID)
+        gain_in, gain_out = ln_in_gain.reshape(1, PAIR), ln_out_gain.reshape(HID // LANES, LANES)
         z4 = z_tile.reshape(ROWS, 2, 2 * HALF, PAIR)
         out_w = [pltpu.VMEM((PAIR, PAIR), BF16), pltpu.VMEM((HID, 1), F32), pltpu.VMEM((PAIR, HID), BF16)]
 
@@ -406,7 +411,7 @@
             last_back_kernel,
             grid=(N_C + N_I,),
             out_shape=jax.ShapeDtypeStruct((ROWS, 2, 2 * HALF, PAIR), BF16),
-            in_specs=specs + [whole(PAIR, PAIR), whole(1, HID), whole(HID, PAIR), first_spec],
+            in_specs=specs + [whole(PAIR, PAIR), whole(HID // LANES, LANES), whole(HID, PAIR), first_spec],
             out_specs=pl.BlockSpec((IB, 2, 2 * HALF, PAIR), lambda s: (jnp.maximum(s - N_C, 0), 0, 0, 0)),
             scratch_shapes=[*out_w, pltpu.VMEM((HID * OPITCH, 2 * HALF), F32)],
             compiler_params=pltpu.CompilerParams(vmem_limit_bytes=VMEM_LIMIT),

time: 326 us -> 324 us (level)
  no operation moved by 1% of the time
where the time goes in v4:
time: 324 us; the launch traced here: 323 us
  Pallas kernels  323 us (100%)
    pallas_call x1, Pallas kernels, per_device(): pl.pallas_call(main_kernel, out_shape=(jax.ShapeDtypeStruct((2, 3, ROWS,...  288 us
    pallas_call x1, Pallas kernels, per_device(): pl.pallas_call(last_back_kernel, grid=(N_C + N_I,), out_shape=jax.ShapeDt...  35.1 us

profile of v4, /device:TPU:5, one launch (start us, length us, event | category | flops | bytes accessed | tf_op | source)
XLA Modules:
  0.0 323.3 jit_solution(14052344959012802340)
XLA Ops:
  0.0 288.2 %exchange_project.1 = (bf16[2,3,128,128,256]{4,3,2,1,0:T(8,128)(2,1)}, bf16[6,256,128,256]{3,2,1,0:T(8,128)(2,1)}, bf16[128,128,256]{2,1,0:T(8,128)(2,1)}, bf16[128,2,64,128]{3,2,1,0:T(8,128)(2,1)}) custom-call(bf16[128,256,128]{2,1,0:T(8,128)(2,1)} %z_ref.1, bf16[128,2,128,128]{3,2,1,0:T(8,128)(2,1)} %bitcast.4, s32[128,256]{1,0:T(8,128)} %mask_in.1, ...), custom_call_target="tpu_custom_call" | custom-call | tf_op jit(solution)/shard_map/exchange_project/pallas_call | solution.py:379
  288.2 35.1 %back.1 = bf16[128,2,128,128]{3,2,1,0:T(8,128)(2,1)} custom-call(bf16[6,256,128,256]{3,2,1,0:T(8,128)(2,1)} %get-tuple-element.8.a0.a1.b0.b1, bf16[6,256,128,256]{3,2,1,0:T(8,128)(2,1)} %get-tuple-element.8.a0.a1.b0.b1, bf16[6,256,128,256]{3,2,1,0:T(8,128)(2,1)} %get-tuple-element.8.a0.a1.b0.b1, bf16[6,256,128,256]{3,2,1,0:T(8,128)(2,1)} %get-tuple-element.8.a0.a1.b0.b1, ...), custom_call_target="tpu_custom_call" | custom-call | tf_op jit(solution)/shard_map/back/pallas_call | solution.py:410

commit v5 on v4

--- a/solution.py
+++ b/solution.py
@@ -16,12 +16,13 @@
 LANES = 128
 FB = 16
 NCH = ROWS // FB
+LAST = NCH - 1
 NH = NCH // 2
 CH = 128
 PITCH = HID + 4
 OPITCH = ROWS + 4
 CB = 32
-IB = 16
+IB = 32
 N_C, N_I = HID // CB, ROWS // IB
 
 
@@ -41,22 +42,28 @@
         xm_ref[r] = (x * m_ref[pl.ds(first + r, 1), :].astype(F32)).astype(BF16)
 
 
-def project_chunk(x_ref, w_ref, o_ref, scr):
-    for r in range(FB):
+def project_rows(x_ref, w_ref, rows, scr, base):
+    for r in rows:
         x = x_ref[r]
         for c in range(0, HID, CH):
             both = jnp.dot(w_ref[2 * c:2 * (c + CH), :], x, preferred_element_type=F32)
             proj = both[:CH]
             val = proj + jnp.tanh(both[CH:]) * proj
             for n in range(COLS // LANES):
-                scr[n, pl.ds(r * PITCH + c, CH), :] = val[:, n * LANES:(n + 1) * LANES]
-
+                scr[pl.ds(base[n] + r * PITCH + c, CH), :] = val[:, n * LANES:(n + 1) * LANES]
+
+
+def write_channels(o_ref, scr, base):
     def channel(c, _):
         for n in range(COLS // LANES):
-            o_ref[c, :, n * LANES:(n + 1) * LANES] = scr[n, pl.ds(c, FB, stride=PITCH), :].astype(BF16)
+            o_ref[c, :, n * LANES:(n + 1) * LANES] = scr[pl.ds(base[n] + c, FB, stride=PITCH), :].astype(BF16)
         return 0
 
     lax.fori_loop(0, HID, channel, 0, unroll=16)
+
+
+def bases(t):
+    return [(t * (COLS // LANES) + n) * FB * PITCH for n in range(COLS // LANES)]
 
 
 def column(row_ref):
@@ -93,7 +100,7 @@
             o_ref[i, :, o_ref.shape[2] - HALF:] = (z + (u + t * u).T).astype(BF16).reshape(2, HALF, PAIR)
             return 0
 
-        lax.fori_loop(0, IB, one_row, 0, unroll=16)
+        lax.fori_loop(0, IB, one_row, 0, unroll=32)
 
 
 def back_specs(half):
@@ -127,6 +134,21 @@
         return pltpu.make_async_remote_copy(src_ref=src, dst_ref=dst, send_sem=send, recv_sem=recv,
                                             device_id=dev, device_id_type=MESH)
 
+    def piece(k, slot, n):
+        return xb.at[k, slot, pl.ds(LAST * FB + n * FB // 2, FB // 2)]
+
+    def p_piece(n):
+        return rdma(piece(0, 0, n), piece(0, 1, n), p_s.at[LAST + n], p_r.at[LAST + n], xdev)
+
+    def q_piece(n):
+        return rdma(piece(1, 1, n), piece(1, 1, n), q_s.at[LAST + n], q_r.at[LAST + n], ydev)
+
+    def s0_piece(n):
+        return rdma(piece(0, mine, n), piece(0, 2, n), s0_s.at[LAST + n], s0_r.at[LAST + n], sdev)
+
+    def s1_piece(n):
+        return rdma(piece(1, mine, n), piece(1, 2, n), s1_s.at[LAST + n], s1_r.at[LAST + n], sdev)
+
     def y(ch):
         return rdma(part(0, 0, ch), part(1, 0, ch), y_s.at[ch], y_r.at[ch], ydev)
 
@@ -165,9 +187,14 @@
         xmstore(ch).wait()
         y(ch).start()
 
-        @pl.when(diag)
+        @pl.when(diag & (ch < LAST))
         def _():
             s0(ch).start()
+
+        @pl.when(diag & (ch == LAST))
+        def _():
+            for n in range(2):
+                s0_piece(n).start()
 
         @pl.when(diag & (ch < NH))
         def _():
@@ -228,30 +255,46 @@
         @pl.when(jnp.logical_not(first_use))
         def _():
             ostore(0, 0, t).wait()
-        project_chunk(xin.at[t], w_ref.at[weight], obuf.at[t % 2], scr)
+        project_rows(xin.at[t], w_ref.at[weight], range(FB), scr, bases(0))
+        write_channels(obuf.at[t % 2], scr, bases(0))
         ostore(dst, block, t).start()
 
     def window1(i, _):
         k, ch = i // NH, i % NH
         y(i).wait_recv()
 
-        @pl.when(diag)
+        @pl.when(diag & (i < LAST))
         def _():
             s1(i).start()
 
+        @pl.when(diag & (i == LAST))
+        def _():
+            for n in range(2):
+                s1_piece(n).start()
+
         @pl.when(diag & (i < NH))
         def _():
             q_relay(i).start()
 
         @pl.when(diag & (i == NH - 1))
         def _():
-            for c in range(NH, NCH):
+            for c in range(NH, LAST):
                 p(c).start()
+            for n in range(2):
+                p_piece(n).start()
 
         @pl.when(diag & (i >= NH))
         def _():
             q_hop(i).wait_recv()
+
+        @pl.when(diag & (i >= NH) & (i < LAST))
+        def _():
             q_hop2(i).start()
+
+        @pl.when(diag & (i == LAST))
+        def _():
+            for n in range(2):
+                q_piece(n).start()
 
         @pl.when(off & (i < NH))
         def _():
@@ -329,25 +372,62 @@
         lax.fori_loop(0, 4, step, 0)
         return 0
 
-    lax.fori_loop(0, NCH - NH, window2, 0)
+    lax.fori_loop(0, LAST - NH, window2, 0)
+
+    def xpiece(k, slot, n, t):
+        return pltpu.make_async_copy(piece(k, slot, n), xin.at[t, pl.ds(n * FB // 2, FB // 2)], xsem.at[t])
+
+    for n in range(2):
+        @pl.when(off)
+        def _(n=n):
+            p_piece(n).wait_recv()
+            s0_piece(n).start()
+            q_piece(n).wait_recv()
+            s1_piece(n).start()
+
+        xpiece(0, mine, n, 0).start()
+        xpiece(1, mine, n, 1).start()
+        for t in range(4):
+            if t == 1:
+                s0_piece(n).wait_recv()
+                xpiece(0, 2, n, 2).start()
+                s1_piece(n).wait_recv()
+                xpiece(1, 2, n, 3).start()
+            xpiece(0, 0, n, t).wait()
+            project_rows(xin.at[t], w_ref.at[1], range(n * FB // 2, (n + 1) * FB // 2), o_scr, bases(t))
+            if n == 1:
+                ostore(0, 0, t).wait()
+                write_channels(obuf.at[t % 2], o_scr, bases(t))
+                ostore(4 + t % 2, (core if t < 2 else 1 - core) * NH + LAST - NH, t).start()
     ostore(0, 0, 0).wait()
     ostore(0, 0, 1).wait()
 
     def drain(ch, _):
         y(ch).wait_send()
-        s0(ch).wait_send()
-        s1(ch).wait_send()
-
-        @pl.when(diag)
+
+        @pl.when(ch < LAST)
+        def _():
+            s0(ch).wait_send()
+            s1(ch).wait_send()
+
+        @pl.when(diag & (ch < LAST))
         def _():
             p(ch).wait_send()
 
-        @pl.when(diag | (ch >= NH))
+        @pl.when((diag & (ch < LAST)) | (off & (ch >= NH)))
         def _():
             q_hop(ch).wait_send()
         return 0
 
     lax.fori_loop(0, NCH, drain, 0)
+    for n in range(2):
+        s0_piece(n).wait_send()
+        s1_piece(n).wait_send()
+
+        @pl.when(diag)
+        def _(n=n):
+            p_piece(n).wait_send()
+            q_piece(n).wait_send()
 
 
 def last_back_kernel(a0, a1, b0, b1, z_ref, x_ref, gate_ref, gain_ref, proj_ref, first_ref, o_ref, gate_t, gain, proj_t, o_scr):
@@ -395,10 +475,10 @@
                 pltpu.VMEM((2, FB, PAIR, COLS), BF16),
                 pltpu.VMEM((4, FB, PAIR, COLS), BF16),
                 pltpu.VMEM((2, HID, FB, COLS), BF16),
-                pltpu.VMEM((COLS // LANES, FB * PITCH, LANES), F32),
+                pltpu.VMEM((COLS // LANES * FB * PITCH, LANES), F32),
                 pltpu.VMEM((HID * OPITCH, 2 * HALF), F32),
                 dma((2,)), dma((2,)), dma((2,)), dma((4,)), dma((2,)),
-            ] + [dma((NCH,))] * 10,
+            ] + [dma((NCH + 1,))] * 10,
             compiler_params=pltpu.CompilerParams(vmem_limit_bytes=VMEM_LIMIT, collective_id=0, has_side_effects=True),
             name='exchange_project',
         )(z_tile, z4, mask_tile, gain_in, proj_a, gate_a, proj_b, gate_b, gate_out, gain_out, proj_out)

time: 324 us -> 320 us (0.988)
  Pallas kernels: 323 us -> 319 us
where the time goes in v5:
time: 320 us; the launch traced here: 319 us
  Pallas kernels  319 us (100%)
    pallas_call x1, Pallas kernels, per_device(): pl.pallas_call(main_kernel, out_shape=(jax.ShapeDtypeStruct((2, 3, ROWS,...  285 us
    pallas_call x1, Pallas kernels, per_device(): pl.pallas_call(last_back_kernel, grid=(N_C + N_I,), out_shape=jax.ShapeDt...  33.9 us

profile of v5, /device:TPU:5, one launch (start us, length us, event | category | flops | bytes accessed | tf_op | source)
XLA Modules:
  0.0 319.2 jit_solution(5706812185878851492)
XLA Ops:
  0.0 285.2 %exchange_project.1 = (bf16[2,3,128,128,256]{4,3,2,1,0:T(8,128)(2,1)}, bf16[6,256,128,256]{3,2,1,0:T(8,128)(2,1)}, bf16[128,128,256]{2,1,0:T(8,128)(2,1)}, bf16[128,2,64,128]{3,2,1,0:T(8,128)(2,1)}) custom-call(bf16[128,256,128]{2,1,0:T(8,128)(2,1)} %z_ref.1, bf16[128,2,128,128]{3,2,1,0:T(8,128)(2,1)} %bitcast.4, s32[128,256]{1,0:T(8,128)} %mask_in.1, ...), custom_call_target="tpu_custom_call" | custom-call | tf_op jit(solution)/shard_map/exchange_project/pallas_call | solution.py:459
  285.2 33.9 %back.1 = bf16[128,2,128,128]{3,2,1,0:T(8,128)(2,1)} custom-call(bf16[6,256,128,256]{3,2,1,0:T(8,128)(2,1)} %get-tuple-element.8.a0.a1.b0.b1, bf16[6,256,128,256]{3,2,1,0:T(8,128)(2,1)} %get-tuple-element.8.a0.a1.b0.b1, bf16[6,256,128,256]{3,2,1,0:T(8,128)(2,1)} %get-tuple-element.8.a0.a1.b0.b1, bf16[6,256,128,256]{3,2,1,0:T(8,128)(2,1)} %get-tuple-element.8.a0.a1.b0.b1, ...), custom_call_target="tpu_custom_call" | custom-call | tf_op jit(solution)/shard_map/back/pallas_call | solution.py:490

commit v6 on v5

--- a/solution.py
+++ b/solution.py
@@ -17,6 +17,8 @@
 FB = 16
 NCH = ROWS // FB
 LAST = NCH - 1
+PIECES = (0, 8, 12, 16)
+N_P = len(PIECES) - 1
 NH = NCH // 2
 CH = 128
 PITCH = HID + 4
@@ -135,7 +137,7 @@
                                             device_id=dev, device_id_type=MESH)
 
     def piece(k, slot, n):
-        return xb.at[k, slot, pl.ds(LAST * FB + n * FB // 2, FB // 2)]
+        return xb.at[k, slot, pl.ds(LAST * FB + PIECES[n], PIECES[n + 1] - PIECES[n])]
 
     def p_piece(n):
         return rdma(piece(0, 0, n), piece(0, 1, n), p_s.at[LAST + n], p_r.at[LAST + n], xdev)
@@ -193,7 +195,7 @@
 
         @pl.when(diag & (ch == LAST))
         def _():
-            for n in range(2):
+            for n in range(N_P):
                 s0_piece(n).start()
 
         @pl.when(diag & (ch < NH))
@@ -208,7 +210,6 @@
     gain = column(gain_in)
     mask = mask_in[...]
     mask_ref[...] = jnp.concatenate([mask[:, n * HALF:(n + 1) * HALF] for n in (0, 2, 1, 3)], axis=1)
-    pl.semaphore_wait(barrier, 3)
 
     def norm_step(ch, _):
         @pl.when(ch + 1 < NCH)
@@ -226,6 +227,7 @@
 
         @pl.when(ch == 0)
         def _():
+            pl.semaphore_wait(barrier, 3)
             publish(0)
 
         @pl.when(ch >= 2)
@@ -269,7 +271,7 @@
 
         @pl.when(diag & (i == LAST))
         def _():
-            for n in range(2):
+            for n in range(N_P):
                 s1_piece(n).start()
 
         @pl.when(diag & (i < NH))
@@ -280,7 +282,7 @@
         def _():
             for c in range(NH, LAST):
                 p(c).start()
-            for n in range(2):
+            for n in range(N_P):
                 p_piece(n).start()
 
         @pl.when(diag & (i >= NH))
@@ -293,7 +295,7 @@
 
         @pl.when(diag & (i == LAST))
         def _():
-            for n in range(2):
+            for n in range(N_P):
                 q_piece(n).start()
 
         @pl.when(off & (i < NH))
@@ -375,17 +377,21 @@
     lax.fori_loop(0, LAST - NH, window2, 0)
 
     def xpiece(k, slot, n, t):
-        return pltpu.make_async_copy(piece(k, slot, n), xin.at[t, pl.ds(n * FB // 2, FB // 2)], xsem.at[t])
-
-    for n in range(2):
+        return pltpu.make_async_copy(piece(k, slot, n), xin.at[t, pl.ds(PIECES[n], PIECES[n + 1] - PIECES[n])], xsem.at[t])
+
+    for n in range(N_P):
         @pl.when(off)
         def _(n=n):
             p_piece(n).wait_recv()
             s0_piece(n).start()
+
+        xpiece(0, mine, n, 0).start()
+
+        @pl.when(off)
+        def _(n=n):
             q_piece(n).wait_recv()
             s1_piece(n).start()
 
-        xpiece(0, mine, n, 0).start()
         xpiece(1, mine, n, 1).start()
         for t in range(4):
             if t == 1:
@@ -394,8 +400,8 @@
                 s1_piece(n).wait_recv()
                 xpiece(1, 2, n, 3).start()
             xpiece(0, 0, n, t).wait()
-            project_rows(xin.at[t], w_ref.at[1], range(n * FB // 2, (n + 1) * FB // 2), o_scr, bases(t))
-            if n == 1:
+            project_rows(xin.at[t], w_ref.at[1], range(PIECES[n], PIECES[n + 1]), o_scr, bases(t))
+            if n == N_P - 1:
                 ostore(0, 0, t).wait()
                 write_channels(obuf.at[t % 2], o_scr, bases(t))
                 ostore(4 + t % 2, (core if t < 2 else 1 - core) * NH + LAST - NH, t).start()
@@ -420,7 +426,7 @@
         return 0
 
     lax.fori_loop(0, NCH, drain, 0)
-    for n in range(2):
+    for n in range(N_P):
         s0_piece(n).wait_send()
         s1_piece(n).wait_send()
 
@@ -478,7 +484,7 @@
                 pltpu.VMEM((COLS // LANES * FB * PITCH, LANES), F32),
                 pltpu.VMEM((HID * OPITCH, 2 * HALF), F32),
                 dma((2,)), dma((2,)), dma((2,)), dma((4,)), dma((2,)),
-            ] + [dma((NCH + 1,))] * 10,
+            ] + [dma((LAST + N_P,))] * 10,
             compiler_params=pltpu.CompilerParams(vmem_limit_bytes=VMEM_LIMIT, collective_id=0, has_side_effects=True),
             name='exchange_project',
         )(z_tile, z4, mask_tile, gain_in, proj_a, gate_a, proj_b, gate_b, gate_out, gain_out, proj_out)

time: 320 us -> 318 us (level)
  no operation moved by 1% of the time
where the time goes in v6:
time: 318 us
  Pallas kernels  318 us (100%)
    pallas_call x1, Pallas kernels, per_device(): pl.pallas_call(main_kernel, out_shape=(jax.ShapeDtypeStruct((2, 3, ROWS,...  284 us
    pallas_call x1, Pallas kernels, per_device(): pl.pallas_call(last_back_kernel, grid=(N_C + N_I,), out_shape=jax.ShapeDt...  33.9 us

profile of v6, /device:TPU:5, one launch (start us, length us, event | category | flops | bytes accessed | tf_op | source)
XLA Modules:
  0.0 317.7 jit_solution(4675280305949509839)
XLA Ops:
  0.0 283.8 %exchange_project.1 = (bf16[2,3,128,128,256]{4,3,2,1,0:T(8,128)(2,1)}, bf16[6,256,128,256]{3,2,1,0:T(8,128)(2,1)}, bf16[128,128,256]{2,1,0:T(8,128)(2,1)}, bf16[128,2,64,128]{3,2,1,0:T(8,128)(2,1)}) custom-call(bf16[128,256,128]{2,1,0:T(8,128)(2,1)} %z_ref.1, bf16[128,2,128,128]{3,2,1,0:T(8,128)(2,1)} %bitcast.4, s32[128,256]{1,0:T(8,128)} %mask_in.1, ...), custom_call_target="tpu_custom_call" | custom-call | tf_op jit(solution)/shard_map/exchange_project/pallas_call | solution.py:465
  283.8 33.9 %back.1 = bf16[128,2,128,128]{3,2,1,0:T(8,128)(2,1)} custom-call(bf16[6,256,128,256]{3,2,1,0:T(8,128)(2,1)} %get-tuple-element.8.a0.a1.b0.b1, bf16[6,256,128,256]{3,2,1,0:T(8,128)(2,1)} %get-tuple-element.8.a0.a1.b0.b1, bf16[6,256,128,256]{3,2,1,0:T(8,128)(2,1)} %get-tuple-element.8.a0.a1.b0.b1, bf16[6,256,128,256]{3,2,1,0:T(8,128)(2,1)} %get-tuple-element.8.a0.a1.b0.b1, ...), custom_call_target="tpu_custom_call" | custom-call | tf_op jit(solution)/shard_map/back/pallas_call | solution.py:496

commit v7 on v6

--- a/solution.py
+++ b/solution.py
@@ -17,7 +17,7 @@
 FB = 16
 NCH = ROWS // FB
 LAST = NCH - 1
-PIECES = (0, 8, 12, 16)
+PIECES = (0, 8, 12, 14, 16)
 N_P = len(PIECES) - 1
 NH = NCH // 2
 CH = 128

time: 318 us -> 319 us (level)
  no operation moved by 1% of the time
where the time goes in v7:
time: 319 us
  Pallas kernels  319 us (100%)
    pallas_call x1, Pallas kernels, per_device(): pl.pallas_call(main_kernel, out_shape=(jax.ShapeDtypeStruct((2, 3, ROWS,...  285 us
    pallas_call x1, Pallas kernels, per_device(): pl.pallas_call(last_back_kernel, grid=(N_C + N_I,), out_shape=jax.ShapeDt...  34 us

profile of v7, /device:TPU:5, one launch (start us, length us, event | category | flops | bytes accessed | tf_op | source)
XLA Modules:
  0.0 318.6 jit_solution(17479182003902590323)
XLA Ops:
  0.0 284.7 %exchange_project.1 = (bf16[2,3,128,128,256]{4,3,2,1,0:T(8,128)(2,1)}, bf16[6,256,128,256]{3,2,1,0:T(8,128)(2,1)}, bf16[128,128,256]{2,1,0:T(8,128)(2,1)}, bf16[128,2,64,128]{3,2,1,0:T(8,128)(2,1)}) custom-call(bf16[128,256,128]{2,1,0:T(8,128)(2,1)} %z_ref.1, bf16[128,2,128,128]{3,2,1,0:T(8,128)(2,1)} %bitcast.4, s32[128,256]{1,0:T(8,128)} %mask_in.1, ...), custom_call_target="tpu_custom_call" | custom-call | tf_op jit(solution)/shard_map/exchange_project/pallas_call | solution.py:465
  284.7 34.0 %back.1 = bf16[128,2,128,128]{3,2,1,0:T(8,128)(2,1)} custom-call(bf16[6,256,128,256]{3,2,1,0:T(8,128)(2,1)} %get-tuple-element.8.a0.a1.b0.b1, bf16[6,256,128,256]{3,2,1,0:T(8,128)(2,1)} %get-tuple-element.8.a0.a1.b0.b1, bf16[6,256,128,256]{3,2,1,0:T(8,128)(2,1)} %get-tuple-element.8.a0.a1.b0.b1, bf16[6,256,128,256]{3,2,1,0:T(8,128)(2,1)} %get-tuple-element.8.a0.a1.b0.b1, ...), custom_call_target="tpu_custom_call" | custom-call | tf_op jit(solution)/shard_map/back/pallas_call | solution.py:496
